TPU v7x, 256 devices: a whole 4x4x8 slice. The times are simulated.
256 devices in a mesh: owner: 16 (over y, x), rows: 16 (over z, core).
Axes of the slice: x: 4, y: 4, z: 8, core: 2. Of those that a mesh axis runs over, the one named last changes fastest.
Arguments:
- train_gate: float32 [64, 2048, 1024], P('owner', 'rows'), may hold values from -0.1875 to 0.1875
- train_up: float32 [64, 2048, 1024], P('owner', 'rows'), may hold values from -0.1875 to 0.1875
- train_down: float32 [64, 1024, 2048], P('owner', None, 'rows'), may hold values from -0.25 to 0.25
- router_weight: float32 [2048, 64], P('rows', 'owner'), may hold values from -0.125 to 0.125
- router_gain: float32 [2048], P('rows'), may hold values from 0.25 to 1.75
Outputs:
- ready_gate: bfloat16 [64, 2048, 1024], P('owner', None, 'rows')
- ready_up: bfloat16 [64, 2048, 1024], P('owner', None, 'rows')
- ready_down: bfloat16 [64, 1024, 2048], P('owner', 'rows')
- scale_gate: float32 [64, 1024], P('owner', 'rows')
- scale_up: float32 [64, 1024], P('owner', 'rows')
- scale_down: float32 [64, 1024], P('owner', 'rows')
- serve_router: bfloat16 [2048, 64], replicated
All inputs are finite; a program needn't handle non-finite values. Where the computation divides by a largest or mean magnitude, that divisor is 1e-20 or more.
Results may differ from a plain program's by a relative error of at most 0.0013.
Values may be sent and summed in bfloat16 or wider, within the bound.
A program may use at most 64 MiB of HBM per device.

v0:
```python
import jax
import jax.numpy as jnp
from jax import lax
from jax.sharding import PartitionSpec as P

D_MODEL = 2048


def copy_for_each(shard, axis):
    size = lax.axis_size(axis)
    return lax.all_to_all(
        jnp.broadcast_to(shard[None], (size, *shard.shape)), axis, 0, 0, tiled=True
    )


def over_copies(shard, axis):
    everything = copy_for_each(shard, axis)
    return jnp.sum(everything, axis=0)


def together(arrays, axis):
    ends = [0]
    for a in arrays:
        ends.append(ends[-1] + a.size)
    total = over_copies(jnp.concatenate([a.ravel() for a in arrays]), axis)
    return tuple((total[b:e].reshape(a.shape) for a, b, e in zip(arrays, ends, ends[1:])))


def sent_together(arrays, axis, split_dim, concat_dim, along):
    ends, at = ([], 0)
    for a in arrays[:-1]:
        at += a.shape[along]
        ends.append(at)
    both = jnp.concatenate(arrays, axis=along)
    return tuple(
        jnp.split(
            lax.all_to_all(both, axis, split_axis=split_dim, concat_axis=concat_dim, tiled=True),
            ends,
            axis=along,
        )
    )


def laid_out(tiles, dim):
    tiles = jnp.moveaxis(tiles, 0, dim)
    dims = tiles.shape
    return tiles.reshape(*dims[:dim], dims[dim] * dims[dim + 1], *dims[dim + 2 :])


def gather_directly(shard, axis, dim):
    tiles = copy_for_each(shard, axis)
    return laid_out(tiles, dim)


def local(train_gate, train_up, train_down, router_weight, router_gain):
    total_gate, total_up, total_down = together(
        (
            jnp.sum(jnp.abs(train_gate), axis=1),
            jnp.sum(jnp.abs(train_up), axis=1),
            jnp.sum(jnp.abs(train_down), axis=2),
        ),
        "rows",
    )
    scale_gate = total_gate / D_MODEL
    scale_up = total_up / D_MODEL
    scale_down = total_down / D_MODEL
    narrow_gate, narrow_up, narrow_down = (
        (train_gate / jnp.expand_dims(scale_gate, 1)).astype(jnp.bfloat16),
        (train_up / jnp.expand_dims(scale_up, 1)).astype(jnp.bfloat16),
        (train_down / jnp.expand_dims(scale_down, 2)).astype(jnp.bfloat16),
    )
    ready_gate, ready_up = sent_together((narrow_gate, narrow_up), "rows", 2, 1, 0)
    ready_down = lax.all_to_all(narrow_down, "rows", split_axis=1, concat_axis=2, tiled=True)
    scale_gate = lax.dynamic_slice_in_dim(
        scale_gate, lax.axis_index("rows") * ready_gate.shape[2], ready_gate.shape[2], axis=1
    )
    scale_up = lax.dynamic_slice_in_dim(
        scale_up, lax.axis_index("rows") * ready_up.shape[2], ready_up.shape[2], axis=1
    )
    scale_down = lax.dynamic_slice_in_dim(
        scale_down, lax.axis_index("rows") * ready_down.shape[1], ready_down.shape[1], axis=1
    )
    part_router = (router_weight * router_gain[:, None]).astype(jnp.bfloat16)
    row_router = gather_directly(part_router, "rows", 0)
    serve_router = gather_directly(row_router, "owner", 1)
    return (ready_gate, ready_up, ready_down, scale_gate, scale_up, scale_down, serve_router)


def solution(mesh):
    return jax.shard_map(
        local,
        mesh=mesh,
        in_specs=(
            P("owner", "rows", None),
            P("owner", "rows", None),
            P("owner", None, "rows"),
            P("rows", "owner"),
            P("rows"),
        ),
        out_specs=(
            P("owner", None, "rows"),
            P("owner", None, "rows"),
            P("owner", "rows", None),
            P("owner", "rows"),
            P("owner", "rows"),
            P("owner", "rows"),
            P(),
        ),
        check_vma=False,
    )
```

profile of v0, /device:TPU:1, one launch (start us, length us, event | category | flops | bytes accessed | tf_op | source)
XLA Modules:
  0.0 150.2 jit_solution(6789340445049301006)
XLA Ops:
  0.6 0.8 multiply_convert_fusion
  1.5 0.6 broadcast_in_dim.9
  2.1 10.0 %all-to-all-start.3 = ((bf16[16,128,4]{1,2,0:T(4,128)(2,1)}), bf16[16,128,4]{1,2,0:T(4,128)(2,1)S(1)}, u32[]{:S(2)}, u32[]{:S(2)}) async-start(bf16[16,128,4]{1,2,0:T(4,128)(2,1)} %broadcast_in_dim.9), calls=%async_computation.3 | async-start | bytes 32768 | tf_op jit(solution)/shard_map/all_to_all | solution.py:11
  12.1 2.0 %abs_reduce_fusion.1 = f32[4,1024]{1,0:T(4,128)S(1)} fusion(f32[4,128,1024]{2,1,0:T(8,128)} %param.6), kind=kLoop, calls=%fused_computation.3 | loop fusion | flops 1044480 | bytes 2113536 | tf_op jit(solution)/shard_map/reduce_sum | solution.py:59
  14.0 0.6 abs_reduce_fusion
  14.9 4.4 %all-to-all-done.3 = bf16[16,128,4]{1,2,0:T(4,128)(2,1)S(1)} async-done(((bf16[16,128,4]{1,2,0:T(4,128)(2,1)}), bf16[16,128,4]{1,2,0:T(4,128)(2,1)S(1)}, u32[]{:S(2)}, u32[]{:S(2)}) %all-to-all-start.3) | async-done | bytes 16416 | tf_op jit(solution)/shard_map/all_to_all | solution.py:11
  19.4 0.6 broadcast_in_dim.8
  20.0 26.0 %all_to_all.49 = f32[16,1,12288]{2,1,0:T(1,128)S(1)} all-to-all(f32[16,1,12288]{2,1,0:T(1,128)S(1)} %broadcast_in_dim.8), channel_id=1, replica_groups=mesh['owner'=16,'rows'=16] {'rows'}, dimensions={0} | all-to-all | bytes 1572864 | tf_op jit(solution)/shard_map/all_to_all | solution.py:11
  46.0 0.8 broadcast_in_dim.11
  46.8 6.8 %all-to-all-start.4 = ((bf16[16,2048,4]{1,2,0:T(4,128)(2,1)}), bf16[16,2048,4]{1,2,0:T(4,128)(2,1)S(1)}, u32[]{:S(2)}, u32[]{:S(2)}) async-start(bf16[16,2048,4]{1,2,0:T(4,128)(2,1)} %broadcast_in_dim.11), calls=%async_computation.4 | async-start | bytes 524288 | tf_op jit(solution)/shard_map/all_to_all | solution.py:11
  53.5 0.5 reduce_sum.39
  54.3 7.2 %fusion = bf16[4,1024,128]{2,0,1:T(4,128)(2,1)} fusion(f32[4,1024,128]{2,1,0:T(8,128)S(1)} %copy-done, f32[4,1024]{0,1:T(8,128)S(1)} %copy.50), kind=kLoop, calls=%fused_computation.5 | loop fusion | flops 1048576 | bytes 3162112 | tf_op jit(solution)/shard_map/convert_element_type | solution.py:70
  61.5 1.2 all-to-all-done.4
  62.7 4.0 %all-to-all-start.2 = ((bf16[4,1024,128]{2,0,1:T(4,128)(2,1)}), bf16[4,1024,128]{2,0,1:T(4,128)(2,1)S(1)}, u32[]{:S(2)}, u32[]{:S(2)}) async-start(bf16[4,1024,128]{2,0,1:T(4,128)(2,1)} %fusion), calls=%async_computation.2 | async-start | bytes 2097152 | tf_op jit(solution)/shard_map/all_to_all | solution.py:73
  66.6 1.9 %copy.44 = f32[4,128,1024]{1,0,2:T(4,128)} copy(f32[4,128,1024]{2,1,0:T(8,128)S(1)} %copy-done.2) | data formatting | bytes 4194304 | tf_op args[0]
  68.5 2.0 %copy.46 = f32[4,128,1024]{1,0,2:T(4,128)S(1)} copy(f32[4,128,1024]{2,1,0:T(8,128)} %param.6) | data formatting | bytes 4194304 | tf_op args[1]
  70.5 1.0 copy.43
  71.6 1.0 copy.45
  72.6 3.6 %divide_convert_fusion.1 = bf16[4,128,1024]{1,0,2:T(4,128)(2,1)S(1)} fusion(f32[4,128,1024]{1,0,2:T(4,128)} %copy.44, f32[4,1024]{0,1:T(8,128)} %copy.43), kind=kLoop, calls=%fused_computation.7 | loop fusion | flops 1048576 | bytes 3162112 | tf_op jit(solution)/shard_map/convert_element_type | solution.py:68
  76.2 2.5 %divide_convert_fusion = bf16[4,128,1024]{1,0,2:T(4,128)(2,1)S(1)} fusion(f32[4,128,1024]{1,0,2:T(4,128)S(1)} %copy.46, f32[4,1024]{0,1:T(8,128)S(1)} %copy-done.3), kind=kLoop, calls=%fused_computation.6 | loop fusion | flops 1048576 | bytes 3162112 | tf_op jit(solution)/shard_map/convert_element_type | solution.py:69
  78.7 2.4 %pad_maximum_fusion = bf16[8,128,1024]{1,0,2:T(8,128)(2,1)} fusion(bf16[4,128,1024]{1,0,2:T(4,128)(2,1)S(1)} %divide_convert_fusion, bf16[4,128,1024]{1,0,2:T(4,128)(2,1)S(1)} %divide_convert_fusion.1), kind=kLoop, calls=%fused_computation | loop fusion | flops 4194304 | bytes 4194304 | tf_op jit(solution)/shard_map/concatenate | solution.py:34
  81.1 13.6 %all-to-all-done.2 = bf16[4,1024,128]{2,0,1:T(4,128)(2,1)S(1)} async-done(((bf16[4,1024,128]{2,0,1:T(4,128)(2,1)}), bf16[4,1024,128]{2,0,1:T(4,128)(2,1)S(1)}, u32[]{:S(2)}, u32[]{:S(2)}) %all-to-all-start.2) | async-done | bytes 1048608 | tf_op jit(solution)/shard_map/all_to_all | solution.py:73
  94.7 3.6 %all-to-all-start.1 = ((bf16[8,128,1024]{1,0,2:T(8,128)(2,1)}), bf16[8,128,1024]{1,0,2:T(8,128)(2,1)S(1)}, u32[]{:S(2)}, u32[]{:S(2)}) async-start(bf16[8,128,1024]{1,0,2:T(8,128)(2,1)} %pad_maximum_fusion), calls=%async_computation.1 | async-start | bytes 4194304 | tf_op jit(solution)/shard_map/all_to_all | solution.py:37
  98.3 0.8 reshape.76
  99.1 0.6 constant_dynamic-slice_fusion
  99.7 0.6 constant_dynamic-slice_fusion.1
  100.4 0.6 constant_dynamic-slice_fusion.2
  101.0 1.6 %copy.52 = bf16[4,64,16,128]{3,2,1,0:T(8,128)(2,1)} copy(bf16[4,64,16,128]{3,0,1,2:T(4,128)(2,1)S(1)} %bitcast.33) | data formatting | bytes 2097152 | tf_op jit(solution)/shard_map/all_to_all | solution.py:73
  102.7 2.3 %all_to_all.41 = bf16[4,64,2048]{2,1,0:T(8,128)(2,1)} reshape(bf16[4,64,16,128]{3,2,1,0:T(8,128)(2,1)} %copy.52) | data formatting | bytes 2097152 | tf_op jit(solution)/shard_map/all_to_all | solution.py:73
  104.9 42.2 %all-to-all-done.1 = bf16[8,128,1024]{1,0,2:T(8,128)(2,1)S(1)} async-done(((bf16[8,128,1024]{1,0,2:T(8,128)(2,1)}), bf16[8,128,1024]{1,0,2:T(8,128)(2,1)S(1)}, u32[]{:S(2)}, u32[]{:S(2)}) %all-to-all-start.1) | async-done | bytes 2097184 | tf_op jit(solution)/shard_map/all_to_all | solution.py:37
  147.7 1.2 copy.70
  148.9 1.2 copy.71
  (19 shorter events, 1.0 us)
Async XLA Ops:
  0.6 13.4 %copy-start = (f32[4,1024,128]{2,1,0:T(8,128)S(1)}, f32[4,1024,128]{2,1,0:T(8,128)}, u32[]{:S(2)}) copy-start(f32[4,1024,128]{2,1,0:T(8,128)} %param.7) | copy-start | bytes 6291460
  2.1 17.3 %all-to-all-start.3 = ((bf16[16,128,4]{1,2,0:T(4,128)(2,1)}), bf16[16,128,4]{1,2,0:T(4,128)(2,1)S(1)}, u32[]{:S(2)}, u32[]{:S(2)}) async-start(bf16[16,128,4]{1,2,0:T(4,128)(2,1)} %broadcast_in_dim.9), calls=%async_computation.3 | async-start | bytes 32768 | tf_op jit(solution)/shard_map/all_to_all | solution.py:11
  12.1 2.6 %copy-start.1 = (f32[4,128,1024]{2,1,0:T(8,128)S(1)}, f32[4,128,1024]{2,1,0:T(8,128)}, u32[]{:S(2)}) copy-start(f32[4,128,1024]{2,1,0:T(8,128)} %param.5) | copy-start | bytes 6291460
  46.8 15.9 %all-to-all-start.4 = ((bf16[16,2048,4]{1,2,0:T(4,128)(2,1)}), bf16[16,2048,4]{1,2,0:T(4,128)(2,1)S(1)}, u32[]{:S(2)}, u32[]{:S(2)}) async-start(bf16[16,2048,4]{1,2,0:T(4,128)(2,1)} %broadcast_in_dim.11), calls=%async_computation.4 | async-start | bytes 524288 | tf_op jit(solution)/shard_map/all_to_all | solution.py:11
  61.5 5.1 %copy-start.2 = (f32[4,128,1024]{2,1,0:T(8,128)S(1)}, f32[4,128,1024]{2,1,0:T(8,128)}, u32[]{:S(2)}) copy-start(f32[4,128,1024]{2,1,0:T(8,128)} %param.5) | copy-start | bytes 6291460
  62.7 32.0 %all-to-all-start.2 = ((bf16[4,1024,128]{2,0,1:T(4,128)(2,1)}), bf16[4,1024,128]{2,0,1:T(4,128)(2,1)S(1)}, u32[]{:S(2)}, u32[]{:S(2)}) async-start(bf16[4,1024,128]{2,0,1:T(4,128)(2,1)} %fusion), calls=%async_computation.2 | async-start | bytes 2097152 | tf_op jit(solution)/shard_map/all_to_all | solution.py:73
  72.6 3.6 %copy-start.3 = (f32[4,1024]{0,1:T(8,128)S(1)}, f32[4,1024]{0,1:T(8,128)}, u32[]{:S(2)}) copy-start(f32[4,1024]{0,1:T(8,128)} %copy.45) | copy-start | bytes 49156
  94.7 52.5 %all-to-all-start.1 = ((bf16[8,128,1024]{1,0,2:T(8,128)(2,1)}), bf16[8,128,1024]{1,0,2:T(8,128)(2,1)S(1)}, u32[]{:S(2)}, u32[]{:S(2)}) async-start(bf16[8,128,1024]{1,0,2:T(8,128)(2,1)} %pad_maximum_fusion), calls=%async_computation.1 | async-start | bytes 4194304 | tf_op jit(solution)/shard_map/all_to_all | solution.py:37
where the time goes:
time: 151 us; the launch traced here: 150 us
  waiting for transfers between devices  61.4 us (41%)
  blocking collectives  26 us (17%)
  starting transfers between devices  24.3 us (16%)
  other arithmetic  19.8 us (13%)
  local copies, waits for them, and re-layouts  17.9 us (12%)
    all_to_all x1, waiting for transfers between devices, sent_together(): lax.all_to_all(both, axis, split_axis=split_dim, concat_axis=concat_dim,...  42.2 us
    all_to_all x1, blocking collectives, copy_for_each(): lax.all_to_all(jnp.broadcast_to(shard[None], (size, *shard.shape)), axis,...  26 us
    all_to_all x2, starting transfers between devices, copy_for_each(): lax.all_to_all(jnp.broadcast_to(shard[None], (size, *shard.shape)), axis,...  16.7 us
    all_to_all x1, waiting for transfers between devices, local(): lax.all_to_all(narrow_down, 'rows', split_axis=1, concat_axis=2, tiled=True)  13.6 us
    convert_element_type x1, other arithmetic, local(): (train_down / jnp.expand_dims(scale_down, 2)).astype(jnp.bfloat16)  7.16 us
    all_to_all x2, waiting for transfers between devices, copy_for_each(): lax.all_to_all(jnp.broadcast_to(shard[None], (size, *shard.shape)), axis,...  5.62 us
    unnamed x12, local copies, waits for them, and re-layouts  4.13 us
    all_to_all x1, starting transfers between devices, local(): lax.all_to_all(narrow_down, 'rows', split_axis=1, concat_axis=2, tiled=True)  3.96 us
  transfers between devices with their start and end apart: 4, of which 4 were waited for; matrix products, arithmetic and copies ran while one was open for 20% of the time, Pallas kernels for 0%

commit v1 on v0

v1 whole, which is shorter than its diff:
```python
import functools

import jax
import jax.numpy as jnp
from jax import lax
from jax.experimental import pallas as pl
from jax.experimental.pallas import tpu as pltpu
from jax.sharding import PartitionSpec as P

D_MODEL = 2048
MESH = pl.DeviceIdType.MESH
F32, BF16 = jnp.float32, jnp.bfloat16

FAR = (4, 3, -3, 2, -2, 1, -1, 0)
PEERS = tuple((dz, dc) for dz in FAR for dc in (0, 1) if (dz, dc) != (0, 0))


def exchange(
    gate, up, down, weight, gain,
    out, scale_gate, scale_up, scale_down, router,
    wide, tall, sent, part0, all0, sums, pieces, total, totals, inverse,
    weight_v, gain_v, mine, column, square,
    load, first_s, first_r, sum_s, sum_r, tot_s, tot_r, main_s, main_r, rt_s, rt_r,
):
    owner, me = lax.axis_index("owner"), lax.axis_index("rows")
    z, c = me // 2, lax.rem(me, 2)
    y, x = owner // 4, lax.rem(owner, 4)

    def peer(dz, dc):
        at = lax.rem(z + dz + 8, 8)
        return at * 2 + (1 - c if dc else c)

    loads = []
    for a in range(12):
        source = (gate, up, down)[a // 4].at[a % 4]
        target = wide.at[a] if a < 8 else tall.at[a - 8]
        loads.append(pltpu.make_async_copy(source, target, load.at[a]))
    small = [
        pltpu.make_async_copy(weight, weight_v, load.at[12]),
        pltpu.make_async_copy(gain, gain_v, load.at[13]),
    ]
    loads[0].start()

    barrier = pltpu.get_barrier_semaphore()
    for dz, dc in PEERS:
        pl.semaphore_signal(barrier, inc=1, device_id={"rows": peer(dz, dc)}, device_id_type=MESH)
    xs = [y * 4 + lax.rem(x + k, 4) for k in (2, 1, 3)]
    ys = [lax.rem(y + k, 4) * 4 + x for k in (2, 1, 3)]
    for o in xs + ys:
        pl.semaphore_signal(barrier, inc=1, device_id={"owner": o}, device_id_type=MESH)
    for copy in loads[1:] + small:
        copy.start()

    eye = lax.broadcasted_iota(jnp.int32, (128, 128), 0) == lax.broadcasted_iota(jnp.int32, (128, 128), 1)

    def wide_sum(a):
        return jnp.sum(jnp.abs(wide[a]), axis=0, keepdims=True)

    loads[0].wait()
    row = wide_sum(0)
    for b in range(8):
        part0[b : b + 1, :] = row[:, b * 128 : (b + 1) * 128]
        pieces[b * 2, 0:1, :] = row[:, b * 128 : (b + 1) * 128]
    pl.semaphore_wait(barrier, len(PEERS) + 6)

    def send(source, target, s, r, to):
        pltpu.make_async_remote_copy(
            src_ref=source, dst_ref=target, send_sem=s, recv_sem=r, device_id=to, device_id_type=MESH
        ).start()

    def finish(ref, sem):
        pltpu.make_async_copy(ref, ref, sem).wait()

    for dz, dc in PEERS:
        send(part0, all0.at[me], first_s, first_r, {"rows": peer(dz, dc)})
    all0[me] = part0[...]

    for a in range(1, 12):
        loads[a].wait()
        if a < 8:
            row = wide_sum(a)
        for b in range(8):
            if a < 8:
                piece = row[:, b * 128 : (b + 1) * 128]
            else:
                column_sum = jnp.sum(jnp.abs(tall[a - 8, b * 128 : (b + 1) * 128, :]), axis=1, keepdims=True)
                piece = jnp.sum(jnp.where(eye, column_sum, 0.0), axis=0, keepdims=True)
            pieces[b * 2 + a // 6, a % 6 : a % 6 + 1, :] = piece
    for dz, dc in PEERS:
        to = peer(dz, dc)
        send(pieces.at[to], sums.at[me], sum_s, sum_r, {"rows": to})
    sums[me] = pieces[me]

    for copy in small:
        copy.wait()
    mine[...] = (weight_v[...] * gain_v[...]).astype(BF16)
    column[me] = mine[...]
    for dz, dc in PEERS:
        send(mine, column.at[me], rt_s.at[0], rt_r.at[0], {"rows": peer(dz, dc)})

    finish(all0.at[pl.ds(0, 15)], first_r)
    first = 1.0 / (jnp.sum(all0[...], axis=0) * (1.0 / D_MODEL))
    for b in range(8):
        inverse[0, b] = first[b : b + 1, :]

    def chunk(a):
        is_wide = not isinstance(a, tuple)
        a = a if is_wide else a[0]
        pending = None
        for dz in FAR:
            at = lax.rem(z + dz + 8, 8)
            rows = pl.ds(pl.multiple_of(at * 128, 128), 128)
            scale = inverse[a, at]
            if is_wide:
                block = (wide[a, :, rows] * scale).astype(BF16).T
            else:
                per_row = jnp.sum(jnp.where(eye, scale, 0.0), axis=1, keepdims=True)
                block = (tall[a - 8, rows, :] * per_row).astype(BF16)
            sent[a, rows, :] = block
            if pending is not None:
                launch(a, pending)
            pending = dz
        launch(a, pending)
        own = sent[a, pl.ds(pl.multiple_of(me * 64, 64), 64), :]
        out[a, :, pl.ds(pl.multiple_of(me * 128, 128), 128)] = own

    def launch(a, dz):
        for dc in (0, 1):
            if (dz, dc) == (0, 0):
                continue
            to = peer(dz, dc)
            send(
                sent.at[a, pl.ds(pl.multiple_of(to * 64, 64), 64), :],
                out.at[a, :, pl.ds(pl.multiple_of(me * 128, 128), 128)],
                main_s.at[a // 4], main_r.at[a // 4], {"rows": to},
            )

    def reduce_sums():
        finish(sums.at[pl.ds(0, 15)], sum_r)
        total[...] = jnp.sum(sums[...], axis=0)
        totals[me] = total[...]
        for dz, dc in PEERS:
            send(total, totals.at[me], tot_s, tot_r, {"rows": peer(dz, dc)})

    reduce_sums()
    chunk(0)

    finish(column.at[pl.ds(0, 15)], rt_r.at[0])
    for r in range(16):
        square[y, x, :, r * 128 : (r + 1) * 128] = column[r]

    finish(totals.at[pl.ds(0, 15)], tot_r)
    for a in range(12):
        for b in range(8):
            if a:
                inverse[a, b] = 1.0 / (totals[b * 2 + a // 6, a % 6 : a % 6 + 1, :] * (1.0 / D_MODEL))

    for o in xs:
        send(square.at[y, x], square.at[y, x], rt_s.at[1], rt_r.at[1], {"owner": o})

    @pl.loop(1, 8)
    def _(a):
        chunk(a)

    finish(square.at[0, pl.ds(0, 3)], rt_r.at[1])
    finish(square.at[0, pl.ds(0, 3)], rt_s.at[1])
    for o in ys:
        send(square.at[y], square.at[y], rt_s.at[2], rt_r.at[2], {"owner": o})

    @pl.loop(8, 12)
    def _(a):
        chunk((a,))

    halves = []
    for h in range(2):
        v = totals[z * 2 + h] * (1.0 / D_MODEL)
        halves.append(jnp.where(c == 1, pltpu.roll(v, 64, 1), v)[:, :64])
    scale_gate[...] = halves[0][:4]
    scale_up[...] = jnp.concatenate([halves[0][4:], halves[1][:2]], axis=0)
    scale_down[...] = halves[1][2:]

    finish(square.at[pl.ds(0, 3)], rt_r.at[2])
    for j in range(4):
        rows16 = jnp.concatenate([square[j, i].astype(F32) for i in range(4)], axis=0)
        router[j * 16 : (j + 1) * 16, :] = rows16.astype(BF16)

    finish(all0.at[pl.ds(0, 15)], first_s)
    finish(sums.at[pl.ds(0, 15)], sum_s)
    finish(totals.at[pl.ds(0, 15)], tot_s)
    finish(column.at[pl.ds(0, 15)], rt_s.at[0])
    finish(square.at[pl.ds(0, 3)], rt_s.at[2])
    for i in range(3):
        finish(out.at[pl.ds(i * 4, 4), :, pl.ds(0, 1920)], main_s.at[i])
        finish(out.at[pl.ds(i * 4, 4), :, pl.ds(0, 1920)], main_r.at[i])


def place(out, scale_gate, scale_up, scale_down, router, *rest):
    outs, sem = rest[:7], rest[7]
    sources = [out.at[pl.ds(0, 4)], out.at[pl.ds(4, 4)], out.at[pl.ds(8, 4)], scale_gate, scale_up, scale_down, router]
    copies = [pltpu.make_async_copy(s, d, sem.at[i]) for i, (s, d) in enumerate(zip(sources, outs))]
    for copy in copies:
        copy.start()
    for copy in copies:
        copy.wait()


def local(train_gate, train_up, train_down, router_weight, router_gain):
    anywhere = pl.BlockSpec(memory_space=pl.ANY)
    vmem = pl.BlockSpec(memory_space=pltpu.VMEM)
    shapes = [((12, 64, 2048), BF16), ((4, 64), F32), ((4, 64), F32), ((4, 64), F32), ((64, 2048), BF16)]
    dma = pltpu.SemaphoreType.DMA
    kept = pl.pallas_call(
        exchange,
        out_shape=[pltpu.VMEM(s, d) for s, d in shapes],
        in_specs=[pl.BlockSpec(memory_space=pltpu.HBM)] * 5,
        out_specs=[vmem] * 5,
        scratch_shapes=[
            pltpu.VMEM((8, 128, 1024), F32),
            pltpu.VMEM((4, 1024, 128), F32),
            pltpu.VMEM((12, 1024, 128), BF16),
            pltpu.VMEM((8, 128), F32),
            pltpu.VMEM((16, 8, 128), F32),
            pltpu.VMEM((16, 6, 128), F32),
            pltpu.VMEM((16, 6, 128), F32),
            pltpu.VMEM((6, 128), F32),
            pltpu.VMEM((16, 6, 128), F32),
            pltpu.VMEM((12, 8, 1, 128), F32),
            pltpu.VMEM((4, 128), F32),
            pltpu.VMEM((1, 128), F32),
            pltpu.VMEM((4, 128), BF16),
            pltpu.VMEM((16, 4, 128), BF16),
            pltpu.VMEM((4, 4, 4, 2048), BF16),
            dma((14,)), dma, dma, dma, dma, dma, dma, dma((3,)), dma((3,)), dma((3,)), dma((3,)),
        ],
        compiler_params=pltpu.CompilerParams(
            collective_id=0, has_side_effects=True, vmem_limit_bytes=58 << 20
        ),
    )(train_gate, train_up, train_down, router_weight.T, router_gain[None])
    outs = [((4, 64, 2048), BF16)] * 3 + [((4, 64), F32)] * 3 + [((64, 2048), BF16)]
    gate, up, down, scale_gate, scale_up, scale_down, router = pl.pallas_call(
        place,
        out_shape=[jax.ShapeDtypeStruct(s, d) for s, d in outs],
        in_specs=[vmem] * 5,
        out_specs=[pl.BlockSpec(memory_space=pltpu.HBM)] * 7,
        scratch_shapes=[dma((7,))],
        compiler_params=pltpu.CompilerParams(vmem_limit_bytes=4 << 20),
    )(*[pltpu.with_memory_space_constraint(k, pltpu.VMEM) for k in kept])
    return (
        jnp.swapaxes(gate, 1, 2), jnp.swapaxes(up, 1, 2), down, scale_gate, scale_up, scale_down, router.T,
    )


def solution(mesh):
    return jax.shard_map(
        local,
        mesh=mesh,
        in_specs=(
            P("owner", "rows", None),
            P("owner", "rows", None),
            P("owner", None, "rows"),
            P("rows", "owner"),
            P("rows"),
        ),
        out_specs=(
            P("owner", None, "rows"),
            P("owner", None, "rows"),
            P("owner", "rows", None),
            P("owner", "rows"),
            P("owner", "rows"),
            P("owner", "rows"),
            P(),
        ),
        check_vma=False,
    )
```

time: 151 us -> 88 us (0.58)
  Pallas kernels: 0 us -> 87.3 us
  waiting for transfers between devices: 61.4 us -> 0 us
  blocking collectives: 26 us -> 0 us
  starting transfers between devices: 24.3 us -> 0 us
  other arithmetic: 19.8 us -> 0 us
  local copies, waits for them, and re-layouts: 17.9 us -> 0 us
    pallas_call x0 -> x2, Pallas kernels: none -> 87.3 us  [the longest x1 85.5 us: local(): pl.pallas_call(exchange, out_shape=[pltpu.VMEM(s, d) for s, d in shapes],...]
    all_to_all x4 -> x0, waiting for transfers between devices: 61.4 us -> none  [the longest x1 42.2 us: sent_together(): lax.all_to_all(both, axis, split_axis=split_dim, concat_axis=concat_dim,...]
    all_to_all x1 -> x0, blocking collectives: 26 us -> none  [copy_for_each(): lax.all_to_all(jnp.broadcast_to(shard[None], (size, *shard.shape)), axis,...]
    all_to_all x4 -> x0, starting transfers between devices: 24.3 us -> none  [the longest x2 16.7 us: copy_for_each(): lax.all_to_all(jnp.broadcast_to(shard[None], (size, *shard.shape)), axis,...]
    convert_element_type x4 -> x0, other arithmetic: 14 us -> none  [the longest x1 7.16 us: local(): (train_down / jnp.expand_dims(scale_down, 2)).astype(jnp.bfloat16)]
    all_to_all x3 -> x0, local copies, waits for them, and re-layouts: 4.21 us -> none  [the longest x2 3.94 us: local(): lax.all_to_all(narrow_down, 'rows', split_axis=1, concat_axis=2, tiled=True)]
    unnamed x12 -> x0, local copies, waits for them, and re-layouts: 4.13 us -> none
    reduce_sum x4 -> x0, other arithmetic: 3.33 us -> none  [the longest x1 1.96 us: local(): jnp.sum(jnp.abs(train_up), axis=1)]
  transfers between devices with their start and end apart: 4 -> 0, of which waited for: 4 -> 0; matrix products, arithmetic and copies ran while one was open for 20% -> 0% of each run, Pallas kernels for 0% -> 0%
where the time goes in v1:
time: 88 us; the launch traced here: 87.9 us
  Pallas kernels  87.3 us (99%)
    pallas_call x1, Pallas kernels, local(): pl.pallas_call(exchange, out_shape=[pltpu.VMEM(s, d) for s, d in shapes],...  85.5 us
    pallas_call x1, Pallas kernels, local(): pl.pallas_call(place, out_shape=[jax.ShapeDtypeStruct(s, d) for s, d in o...  1.81 us

profile of v1, /device:TPU:1, one launch (start us, length us, event | category | flops | bytes accessed | tf_op | source)
XLA Modules:
  0.0 87.9 jit_solution(16174527455513302247)
XLA Ops:
  0.6 85.5 %shard_map.108 = (bf16[12,64,2048]{2,1,0:T(8,128)(2,1)S(1)}, f32[4,64]{1,0:T(4,128)S(1)}, f32[4,64]{1,0:T(4,128)S(1)}, f32[4,64]{1,0:T(4,128)S(1)}, bf16[64,2048]{1,0:T(8,128)(2,1)S(1)}) custom-call(f32[4,128,1024]{2,1,0:T(8,128)} %gate.1, f32[4,128,1024]{2,1,0:T(8,128)} %up.1, f32[4,1024,128]{2,1,0:T(8,128)} %down.1, f32[4,128]{1,0:T(4,128)} %bitcast.5, ...), custom_call_target="tpu_custom_call" | custom-call | tf_op jit(solution)/shard_map/pallas_call | solution.py:212
  86.1 1.8 %shard_map.109 = (bf16[4,64,2048]{2,1,0:T(8,128)(2,1)}, bf16[4,64,2048]{2,1,0:T(8,128)(2,1)}, bf16[4,64,2048]{2,1,0:T(8,128)(2,1)}, f32[4,64]{1,0:T(4,128)}, f32...) custom-call(bf16[12,64,2048]{2,1,0:T(8,128)(2,1)S(1)} %get-tuple-element.19.out, ...), custom_call_target="tpu_custom_call" | custom-call | tf_op jit(solution)/shard_map/pallas_call | solution.py:240

commit v2 on v1

--- a/solution.py
+++ b/solution.py
@@ -11,7 +11,9 @@
 MESH = pl.DeviceIdType.MESH
 F32, BF16 = jnp.float32, jnp.bfloat16
 
+RAW = 2
 FAR = (4, 3, -3, 2, -2, 1, -1, 0)
+NEAR = ((1, 0), (1, 1), (-1, 0), (-1, 1))
 PEERS = tuple((dz, dc) for dz in FAR for dc in (0, 1) if (dz, dc) != (0, 0))
 
 
@@ -19,8 +21,8 @@
     gate, up, down, weight, gain,
     out, scale_gate, scale_up, scale_down, router,
     wide, tall, sent, part0, all0, sums, pieces, total, totals, inverse,
-    weight_v, gain_v, mine, column, square,
-    load, first_s, first_r, sum_s, sum_r, tot_s, tot_r, main_s, main_r, rt_s, rt_r,
+    weight_v, gain_v, mine, column, square, plain,
+    load, first_s, first_r, sum_s, sum_r, tot_s, tot_r, main_s, main_r, rt_s, rt_r, raw_s, raw_r, both_s, both_r,
 ):
     owner, me = lax.axis_index("owner"), lax.axis_index("rows")
     z, c = me // 2, lax.rem(me, 2)
@@ -61,6 +63,20 @@
     for b in range(8):
         part0[b : b + 1, :] = row[:, b * 128 : (b + 1) * 128]
         pieces[b * 2, 0:1, :] = row[:, b * 128 : (b + 1) * 128]
+    def add_up():
+        for a in range(1, 12):
+            loads[a].wait()
+            if a < 8:
+                row = wide_sum(a)
+            for b in range(8):
+                if a < 8:
+                    piece = row[:, b * 128 : (b + 1) * 128]
+                else:
+                    column_sum = jnp.sum(jnp.abs(tall[a - 8, b * 128 : (b + 1) * 128, :]), axis=1, keepdims=True)
+                    piece = jnp.sum(jnp.where(eye, column_sum, 0.0), axis=0, keepdims=True)
+                pieces[b * 2 + a // 6, a % 6 : a % 6 + 1, :] = piece
+
+    pl.when(z < 4)(add_up)
     pl.semaphore_wait(barrier, len(PEERS) + 6)
 
     def send(source, target, s, r, to):
@@ -75,21 +91,16 @@
         send(part0, all0.at[me], first_s, first_r, {"rows": peer(dz, dc)})
     all0[me] = part0[...]
 
-    for a in range(1, 12):
-        loads[a].wait()
-        if a < 8:
-            row = wide_sum(a)
-        for b in range(8):
-            if a < 8:
-                piece = row[:, b * 128 : (b + 1) * 128]
-            else:
-                column_sum = jnp.sum(jnp.abs(tall[a - 8, b * 128 : (b + 1) * 128, :]), axis=1, keepdims=True)
-                piece = jnp.sum(jnp.where(eye, column_sum, 0.0), axis=0, keepdims=True)
-            pieces[b * 2 + a // 6, a % 6 : a % 6 + 1, :] = piece
+    pl.when(z >= 4)(add_up)
     for dz, dc in PEERS:
         to = peer(dz, dc)
         send(pieces.at[to], sums.at[me], sum_s, sum_r, {"rows": to})
     sums[me] = pieces[me]
+
+    for k, (dz, dc) in enumerate(NEAR):
+        to = peer(dz, dc)
+        rows = pl.ds(pl.multiple_of(to * 64, 64), 64)
+        send(tall.at[pl.ds(0, RAW), rows, :], plain.at[k], raw_s, raw_r, {"rows": to})
 
     for copy in small:
         copy.wait()
@@ -103,11 +114,13 @@
     for b in range(8):
         inverse[0, b] = first[b : b + 1, :]
 
-    def chunk(a):
+    def chunk(a, raw=False):
         is_wide = not isinstance(a, tuple)
         a = a if is_wide else a[0]
         pending = None
         for dz in FAR:
+            if raw and abs(dz) == 1:
+                continue
             at = lax.rem(z + dz + 8, 8)
             rows = pl.ds(pl.multiple_of(at * 128, 128), 128)
             scale = inverse[a, at]
@@ -125,6 +138,7 @@
         out[a, :, pl.ds(pl.multiple_of(me * 128, 128), 128)] = own
 
     def launch(a, dz):
+        group = a // 4 + (a >= 8 + RAW)
         for dc in (0, 1):
             if (dz, dc) == (0, 0):
                 continue
@@ -132,15 +146,15 @@
             send(
                 sent.at[a, pl.ds(pl.multiple_of(to * 64, 64), 64), :],
                 out.at[a, :, pl.ds(pl.multiple_of(me * 128, 128), 128)],
-                main_s.at[a // 4], main_r.at[a // 4], {"rows": to},
+                main_s.at[group], main_r.at[group], {"rows": to},
             )
 
     def reduce_sums():
         finish(sums.at[pl.ds(0, 15)], sum_r)
         total[...] = jnp.sum(sums[...], axis=0)
-        totals[me] = total[...]
-        for dz, dc in PEERS:
-            send(total, totals.at[me], tot_s, tot_r, {"rows": peer(dz, dc)})
+        totals[c, z] = total[...]
+        for dz in FAR[:-1]:
+            send(total, totals.at[c, z], tot_s, tot_r, {"rows": peer(dz, 0)})
 
     reduce_sums()
     chunk(0)
@@ -149,11 +163,13 @@
     for r in range(16):
         square[y, x, :, r * 128 : (r + 1) * 128] = column[r]
 
-    finish(totals.at[pl.ds(0, 15)], tot_r)
+    finish(totals.at[0, pl.ds(0, 7)], tot_r)
+    send(totals.at[c], totals.at[c], both_s, both_r, {"rows": peer(0, 1)})
+    finish(totals.at[0], both_r)
     for a in range(12):
         for b in range(8):
             if a:
-                inverse[a, b] = 1.0 / (totals[b * 2 + a // 6, a % 6 : a % 6 + 1, :] * (1.0 / D_MODEL))
+                inverse[a, b] = 1.0 / (totals[a // 6, b, a % 6 : a % 6 + 1, :] * (1.0 / D_MODEL))
 
     for o in xs:
         send(square.at[y, x], square.at[y, x], rt_s.at[1], rt_r.at[1], {"owner": o})
@@ -167,18 +183,31 @@
     for o in ys:
         send(square.at[y], square.at[y], rt_s.at[2], rt_r.at[2], {"owner": o})
 
-    @pl.loop(8, 12)
+    @pl.loop(8, 8 + RAW)
+    def _(a):
+        chunk((a,), raw=True)
+
+    @pl.loop(8 + RAW, 12)
     def _(a):
         chunk((a,))
 
     halves = []
     for h in range(2):
-        v = totals[z * 2 + h] * (1.0 / D_MODEL)
+        v = totals[h, z] * (1.0 / D_MODEL)
         halves.append(jnp.where(c == 1, pltpu.roll(v, 64, 1), v)[:, :64])
     scale_gate[...] = halves[0][:4]
     scale_up[...] = jnp.concatenate([halves[0][4:], halves[1][:2]], axis=0)
     scale_down[...] = halves[1][2:]
 
+    finish(plain, raw_r)
+    for e in range(RAW):
+        last = 1.0 / halves[1][2 + e : 3 + e]
+        last = jnp.concatenate([last, last], axis=1)
+        per_row = jnp.sum(jnp.where(eye, last, 0.0), axis=1, keepdims=True)[:64]
+        for k, (dz, dc) in enumerate(NEAR):
+            lanes = pl.ds(pl.multiple_of(peer(-dz, dc) * 128, 128), 128)
+            out[8 + e, :, lanes] = (plain[k, e] * per_row).astype(BF16)
+
     finish(square.at[pl.ds(0, 3)], rt_r.at[2])
     for j in range(4):
         rows16 = jnp.concatenate([square[j, i].astype(F32) for i in range(4)], axis=0)
@@ -186,12 +215,18 @@
 
     finish(all0.at[pl.ds(0, 15)], first_s)
     finish(sums.at[pl.ds(0, 15)], sum_s)
-    finish(totals.at[pl.ds(0, 15)], tot_s)
+    finish(totals.at[0, pl.ds(0, 7)], tot_s)
+    finish(totals.at[0], both_s)
     finish(column.at[pl.ds(0, 15)], rt_s.at[0])
     finish(square.at[pl.ds(0, 3)], rt_s.at[2])
-    for i in range(3):
-        finish(out.at[pl.ds(i * 4, 4), :, pl.ds(0, 1920)], main_s.at[i])
-        finish(out.at[pl.ds(i * 4, 4), :, pl.ds(0, 1920)], main_r.at[i])
+    finish(plain, raw_s)
+    everything = [
+        out.at[pl.ds(0, 4), :, pl.ds(0, 1920)], out.at[pl.ds(4, 4), :, pl.ds(0, 1920)],
+        out.at[pl.ds(8, RAW), :, pl.ds(0, 1408)], out.at[pl.ds(8 + RAW, 4 - RAW), :, pl.ds(0, 1920)],
+    ]
+    for i, ref in enumerate(everything):
+        finish(ref, main_s.at[i])
+        finish(ref, main_r.at[i])
 
 
 def place(out, scale_gate, scale_up, scale_down, router, *rest):
@@ -223,14 +258,15 @@
             pltpu.VMEM((16, 6, 128), F32),
             pltpu.VMEM((16, 6, 128), F32),
             pltpu.VMEM((6, 128), F32),
-            pltpu.VMEM((16, 6, 128), F32),
+            pltpu.VMEM((2, 8, 6, 128), F32),
             pltpu.VMEM((12, 8, 1, 128), F32),
             pltpu.VMEM((4, 128), F32),
             pltpu.VMEM((1, 128), F32),
             pltpu.VMEM((4, 128), BF16),
             pltpu.VMEM((16, 4, 128), BF16),
             pltpu.VMEM((4, 4, 4, 2048), BF16),
-            dma((14,)), dma, dma, dma, dma, dma, dma, dma((3,)), dma((3,)), dma((3,)), dma((3,)),
+            pltpu.VMEM((4, RAW, 64, 128), F32),
+            dma((14,)), dma, dma, dma, dma, dma, dma, dma((4,)), dma((4,)), dma((3,)), dma((3,)), dma, dma, dma, dma,
         ],
         compiler_params=pltpu.CompilerParams(
             collective_id=0, has_side_effects=True, vmem_limit_bytes=58 << 20

time: 88 us -> 86.3 us (0.981)
  Pallas kernels: 87.3 us -> 85.6 us
    pallas_call x1, Pallas kernels: 85.5 us -> 83.8 us  [local(): pl.pallas_call(exchange, out_shape=[pltpu.VMEM(s, d) for s, d in shapes],...]
where the time goes in v2:
time: 86.3 us; the launch traced here: 86.2 us
  Pallas kernels  85.6 us (99%)
    pallas_call x1, Pallas kernels, local(): pl.pallas_call(exchange, out_shape=[pltpu.VMEM(s, d) for s, d in shapes],...  83.8 us
    pallas_call x1, Pallas kernels, local(): pl.pallas_call(place, out_shape=[jax.ShapeDtypeStruct(s, d) for s, d in o...  1.81 us

profile of v2, /device:TPU:1, one launch (start us, length us, event | category | flops | bytes accessed | tf_op | source)
XLA Modules:
  0.0 86.2 jit_solution(10943319318815677663)
XLA Ops:
  0.6 83.8 %shard_map.108 = (bf16[12,64,2048]{2,1,0:T(8,128)(2,1)S(1)}, f32[4,64]{1,0:T(4,128)S(1)}, f32[4,64]{1,0:T(4,128)S(1)}, f32[4,64]{1,0:T(4,128)S(1)}, bf16[64,2048]{1,0:T(8,128)(2,1)S(1)}) custom-call(f32[4,128,1024]{2,1,0:T(8,128)} %gate.1, f32[4,128,1024]{2,1,0:T(8,128)} %up.1, f32[4,1024,128]{2,1,0:T(8,128)} %down.1, f32[4,128]{1,0:T(4,128)} %bitcast.5, ...), custom_call_target="tpu_custom_call" | custom-call | tf_op jit(solution)/shard_map/pallas_call | solution.py:247
  84.4 1.8 %shard_map.109 = (bf16[4,64,2048]{2,1,0:T(8,128)(2,1)}, bf16[4,64,2048]{2,1,0:T(8,128)(2,1)}, bf16[4,64,2048]{2,1,0:T(8,128)(2,1)}, f32[4,64]{1,0:T(4,128)}, f32...) custom-call(bf16[12,64,2048]{2,1,0:T(8,128)(2,1)S(1)} %get-tuple-element.19.out, ...), custom_call_target="tpu_custom_call" | custom-call | tf_op jit(solution)/shard_map/pallas_call | solution.py:276
